TPU v7x, 256 devices: a 4x2x16 block of a 4x16x16 slice. The times are simulated.
256 devices in a mesh: groups: 2 (over y), dp: 32 (over z, core), expert: 4 (over x).
Axes of the slice: x: 4, y: 2, z: 16, core: 2. Of those that a mesh axis runs over, the one named last changes fastest.
The devices are a block of a 4x16x16 slice.
Arguments:
- queries: bfloat16 [2, 1024, 32, 128], P(None, ('groups', 'dp'), 'expert'), parts along dimension 1, may hold values from -6 to 6
- fresh_kv: bfloat16 [2, 1024, 4, 256], P(None, ('groups', 'dp'), 'expert'), parts along dimension 1, may hold values from -6 to 6
- kv_pool: bfloat16 [20480, 16, 4, 256], P(('groups', 'dp'), None, 'expert'), parts along dimension 0, may hold values from -6 to 6
- page_table: int32 [1024, 305], P(('groups', 'dp')), parts along dimension 0, may hold values from -1 to 319, as said below
- context_lengths: int32 [1024], P(('groups', 'dp')), parts along dimension 0, may hold values from 1 to 4880, as said below
- residual: bfloat16 [2, 1024, 4096], P(None, ('groups', 'dp'), 'expert'), parts along dimension 1, may hold values from -16 to 16
- out_weight: bfloat16 [4096, 4096], P('expert', 'dp'), may hold values from -0.09375 to 0.09375
- norm_gain: float32 [4096], P('expert'), may hold values from 0.1 to 1.9
- expert_ids: int32 [2, 1024, 8], P(None, ('groups', 'dp')), parts along dimension 1, may hold values from 0 to 63, all different within a row; in each aligned block of 16 rows (0 to 15, 16 to 31, ..., all dimensions but the last counted through in order) at most 5 rows name the same one
- route_weights: float32 [2, 1024, 8], P(None, ('groups', 'dp')), parts along dimension 1, may hold values from 0.1 to 1
- gate_up: bfloat16 [64, 2, 4096, 768], P('dp', None, 'expert'), may hold values from -0.09375 to 0.09375
- down_proj: bfloat16 [64, 768, 4096], P('dp', None, 'expert'), may hold values from -0.21875 to 0.21875
Outputs:
- layer_out: bfloat16 [2, 1024, 4096], P(None, ('groups', 'dp'), 'expert'), parts along dimension 1
There are 2 independent parts, one for each index of `groups`. A program takes and returns all parts, laid end to end along the dimension named above; an argument that names none is the same for every part. Nothing has to cross between parts.
Inputs may be any that keep to these rules, and one draw needn't show every extreme that they name: `page_table`: entries 0 to ceil(context_lengths[i] / 16) - 1 of a row name distinct pages, no page is named twice within the 16 requests of one block, and later entries are -1. The requests of one block hold at most 320 pages together; in every draw some block holds exactly 320, and some request holds exactly 305 pages. `context_lengths`: every request holds at least one cached token; in every draw some request holds exactly 4880. `expert_ids`: within the rows of one device (16 requests of one step) no expert is named by more than 5 rows.
All inputs are finite; a program needn't handle non-finite values.
Results may differ from a plain program's by a relative error of at most 0.005.
Values may be sent and summed in bfloat16 or wider, within the bound.
A program may use at most 64 MiB of HBM per device.

v0:
```python
import math
import jax
import jax.numpy as jnp
from jax import lax
from jax.sharding import PartitionSpec as P

NEG = -1e30
EPS = 1e-06
EXACT = lax.Precision.HIGHEST


def in_blocks(array, dim, length):
    before, after = (array.shape[:dim], array.shape[dim + 1 :])
    return jnp.moveaxis(array.reshape(*before, length, -1, *after), dim, 0)


def summed_on_arrival(array, axis, dim):
    length = lax.axis_size(axis)
    pieces = lax.all_to_all(in_blocks(array, dim, length), axis, 0, 0, tiled=True)
    return jnp.sum(pieces.astype(jnp.float32), axis=0)


def in_one_piece(arrays, axis, dim, along):
    both = jnp.concatenate(arrays, axis=along)
    whole, at, outs = (summed_on_arrival(both, axis, dim), 0, [])
    for a in arrays:
        outs.append(lax.slice_in_dim(whole, at, at + a.shape[along], axis=along))
        at += a.shape[along]
    return tuple(outs)


def page_owners(table, lengths, pool_pages, page_len):
    pages = jnp.arange(pool_pages, dtype=jnp.int32)
    matches = table[:, :, None] == pages[None, None, :]
    ownership = jnp.any(matches, axis=1)
    slot_index = jnp.arange(table.shape[1], dtype=jnp.int32)
    position = jnp.sum(jnp.where(matches, slot_index[None, :, None], 0), axis=(0, 1))
    owner_length = jnp.sum(jnp.where(ownership, lengths[:, None], 0), axis=0)
    live_count = jnp.clip(owner_length - position * page_len, 0, page_len)
    return (ownership, live_count)


def attend(query_block, fresh_block, pool_block, table_block, length_block):
    step_count, req_count, head_count, head_width = query_block.shape
    pool_pages, page_len, kv_heads, _ = pool_block.shape
    group_size = head_count // kv_heads
    score_scale = 1.0 / math.sqrt(head_width)
    ownership, live_count = page_owners(table_block, length_block, pool_pages, page_len)
    owned_f = ownership.astype(jnp.float32)
    grouped = query_block.reshape(step_count, req_count, kv_heads, group_size, head_width)
    page_query = jnp.einsum(
        "rp,srkgd->pskgd",
        ownership.astype(jnp.bfloat16),
        grouped,
        preferred_element_type=jnp.float32,
    ).astype(jnp.bfloat16)
    key_rows = pool_block[..., :head_width]
    value_rows = pool_block[..., head_width:]
    page_scores = (
        jnp.einsum("pskgd,ptkd->pskgt", page_query, key_rows, preferred_element_type=jnp.float32)
        * score_scale
    )
    in_page = jnp.arange(page_len)[None, :] < live_count[:, None]
    page_scores = jnp.where(in_page[:, None, None, None, :], page_scores, NEG)
    fresh_keys = fresh_block[..., :head_width]
    fresh_values = fresh_block[..., head_width:]
    fresh_scores = (
        jnp.einsum("srkgd,urkd->srkgu", grouped, fresh_keys, preferred_element_type=jnp.float32)
        * score_scale
    )
    causal = jnp.arange(step_count)[:, None] >= jnp.arange(step_count)[None, :]
    fresh_scores = jnp.where(causal[:, None, None, None, :], fresh_scores, NEG)
    page_best = jnp.max(page_scores, axis=4)
    row_best = jnp.max(jnp.where(ownership[:, :, None, None, None], page_best[None], NEG), axis=1)
    row_best = jnp.maximum(row_best, jnp.moveaxis(jnp.max(fresh_scores, axis=4), 0, 1))
    owner_best = jnp.einsum("rp,rskg->pskg", owned_f, row_best, precision=EXACT)
    page_probs = jnp.exp(page_scores - owner_best[..., None])
    page_sum = jnp.sum(page_probs, axis=4)
    page_acc = jnp.einsum(
        "pskgt,ptkd->pskgd",
        page_probs.astype(jnp.bfloat16),
        value_rows,
        preferred_element_type=jnp.float32,
    )
    denominator = jnp.einsum("rp,pskg->rskg", owned_f, page_sum, precision=EXACT)
    numerator = jnp.einsum("rp,pskgd->rskgd", owned_f, page_acc, precision=EXACT)
    fresh_probs = jnp.exp(fresh_scores - jnp.moveaxis(row_best, 1, 0)[..., None])
    denominator = denominator + jnp.moveaxis(jnp.sum(fresh_probs, axis=4), 0, 1)
    numerator = numerator + jnp.einsum(
        "srkgu,urkd->rskgd",
        fresh_probs.astype(jnp.bfloat16),
        fresh_values,
        preferred_element_type=jnp.float32,
    )
    attended = jnp.moveaxis(numerator / denominator[..., None], 1, 0)
    return attended.reshape(step_count, req_count, head_count * head_width).astype(jnp.bfloat16)


def dispatch_keys(expert_ids, expert_total, local_experts, dp_count, capacity):
    step_count = expert_ids.shape[0]
    catalog = jnp.arange(expert_total, dtype=jnp.int32)
    named_mask = jnp.any(expert_ids[..., None] == catalog, axis=2).astype(jnp.int32)
    earlier = jnp.cumsum(named_mask, axis=1) - named_mask
    slot_rank = jnp.take_along_axis(earlier, expert_ids, axis=2)
    owner_index = expert_ids // local_experts
    local_index = expert_ids % local_experts
    step_index = jnp.arange(step_count, dtype=jnp.int32)[:, None, None]
    return ((local_index * dp_count + owner_index) * step_count + step_index) * capacity + slot_rank


def body(
    queries,
    fresh_kv,
    kv_pool,
    page_table,
    context_lengths,
    residual,
    out_weight,
    norm_gain,
    expert_ids,
    route_weights,
    gate_up,
    down_proj,
):
    attended = attend(queries, fresh_kv, kv_pool, page_table, context_lengths)
    step_count, req_count, head_cols = attended.shape
    flat_attended = attended.reshape(step_count * req_count, head_cols)
    partial_out = jnp.dot(
        flat_attended,
        lax.all_gather(out_weight, "dp", axis=1, tiled=True),
        preferred_element_type=jnp.float32,
    )
    projected = summed_on_arrival(partial_out.astype(jnp.bfloat16), "expert", 1)
    quarter = projected.shape[1]
    stream = residual.astype(jnp.float32).reshape(step_count * req_count, quarter) + projected
    squares = lax.psum(jnp.sum(stream * stream, axis=1), "expert")
    model_width = quarter * lax.axis_size("expert")
    inverse = lax.rsqrt(squares / model_width + EPS)
    normed = (stream * inverse[:, None] * norm_gain[None, :]).astype(jnp.bfloat16)
    dp_count = lax.axis_size("dp")
    local_experts = gate_up.shape[0]
    expert_total = local_experts * dp_count
    top_count = expert_ids.shape[2]
    capacity = min(
        req_count, max(2, (5 * req_count * top_count + 2 * expert_total - 1) // (2 * expert_total))
    )
    slot_keys = dispatch_keys(expert_ids, expert_total, local_experts, dp_count, capacity)
    slot_total = local_experts * dp_count * step_count * capacity
    slot_ids = jnp.arange(slot_total, dtype=jnp.int32)
    chosen = slot_keys.reshape(step_count * req_count, top_count)[None] == slot_ids[:, None, None]
    selector = jnp.any(chosen, axis=2).astype(jnp.bfloat16)
    outgoing = jnp.dot(selector, normed, preferred_element_type=jnp.float32).astype(jnp.bfloat16)
    outgoing = outgoing.reshape(local_experts, dp_count, step_count * capacity, quarter)
    incoming = lax.all_to_all(outgoing, "dp", split_axis=1, concat_axis=1, tiled=True)
    expert_rows = incoming.reshape(local_experts, dp_count * step_count * capacity, quarter)
    gate_part = jnp.einsum(
        "jmd,jdh->jmh", expert_rows, gate_up[:, 0], preferred_element_type=jnp.float32
    )
    up_part = jnp.einsum(
        "jmd,jdh->jmh", expert_rows, gate_up[:, 1], preferred_element_type=jnp.float32
    )
    gate_share, up_share = in_one_piece(
        (gate_part.astype(jnp.bfloat16), up_part.astype(jnp.bfloat16)), "expert", 2, 0
    )
    active_share = (jax.nn.silu(gate_share) * up_share).astype(jnp.bfloat16)
    activated = lax.all_gather(active_share, "expert", axis=2, tiled=True)
    expert_out = jnp.einsum(
        "jmh,jhd->jmd", activated, down_proj, preferred_element_type=jnp.float32
    ).astype(jnp.bfloat16)
    expert_out = expert_out.reshape(local_experts, dp_count, step_count * capacity, quarter)
    returned = lax.all_to_all(expert_out, "dp", split_axis=1, concat_axis=1, tiled=True)
    returned = returned.reshape(slot_total, quarter)
    picked = returned[slot_keys].astype(jnp.float32)
    share = route_weights / jnp.sum(route_weights, axis=2, keepdims=True)
    mixture = jnp.sum(share[..., None] * picked, axis=2)
    return (stream.reshape(step_count, req_count, quarter) + mixture).astype(jnp.bfloat16)


def solution(mesh):
    return jax.shard_map(
        body,
        mesh=mesh,
        in_specs=(
            P(None, ("groups", "dp"), "expert", None),
            P(None, ("groups", "dp"), "expert", None),
            P(("groups", "dp"), None, "expert", None),
            P(("groups", "dp"), None),
            P(("groups", "dp")),
            P(None, ("groups", "dp"), "expert"),
            P("expert", "dp"),
            P("expert"),
            P(None, ("groups", "dp"), None),
            P(None, ("groups", "dp"), None),
            P("dp", None, "expert", None),
            P("dp", None, "expert"),
        ),
        out_specs=P(None, ("groups", "dp"), "expert"),
        check_vma=False,
    )
```

profile of v0, /device:TPU:33, one launch (start us, length us, event | category | flops | bytes accessed | tf_op | source)
XLA Modules:
  0.0 385.2 jit_solution(539590098517076246)
XLA Ops:
  10.3 1.5 select_reduce_fusion
  11.9 1.4 convolution_convert_fusion.1
  13.3 4.5 %fusion.12 = (f32[320,2,8]{2,1,0:T(2,128)S(1)}, f32[320,2,8,16]{3,2,1,0:T(8,128)}) fusion(pred[320,16]{1,0:T(8,128)(4,1)S(1)} %iota_compare_fusion.2, bf16[320,16,1,256]{3,1,0,2:T(8,128)(2,1)} %bitcast.199, bf16[320,2,8,128]{3,0,2,1:T(8,128)(2,1)S(1)} %convolution_convert_fusion.1), kind=kOutput, calls=%fused_computation.20 | convolution fusion | flops 21212160 | bytes 2974720 | tf_op jit(solution)/shard_map/pskgd,ptkd->pskgt/dot_general | solution.py:60
  20.0 1.9 fusion.86
  24.2 3.9 %fusion.10 = f32[320,2,8]{2,1,0:T(2,128)} fusion(f32[320,2,8,16]{3,2,1,0:T(8,128)} %get-tuple-element.12, f32[320,2,8]{2,1,0:T(2,128)S(1)} %copy.127, pred[320,16]{1,0:T(8,128)(4,1)S(1)} %iota_compare_fusion.2), kind=kLoop, calls=%fused_computation.18 | loop fusion | flops 322560 | bytes 373760 | tf_op jit(solution)/shard_map/reduce_sum | solution.py:78
  28.1 1.7 copy.132
  33.9 3.0 fusion.20
  37.0 1.6 fusion.42
  39.0 2.4 gather_fusion.1
  41.6 76.4 %all-gather.2.cloned.1.call-done = bf16[1024,4096]{1,0:T(8,128)(2,1)} async-done(((bf16[1024,128]{1,0:T(8,128)(2,1)}), bf16[1024,4096]{1,0:T(8,128)(2,1)}) %all-gather.2.cloned.1.call-update) | async-done | bytes 8388624 | tf_op jit(solution)/shard_map/all_gather | solution.py:130
  118.0 4.9 %convolution_convert_fusion = bf16[32,4096]{1,0:T(8,128)(2,1)S(1)} fusion(bf16[1024,4096]{1,0:T(8,128)(2,1)} %all-gather.2.cloned.1.call-done, bf16[4,8,8,128]{3,2,1,0:T(8,128)(2,1)S(1)} %bitcast.201), kind=kOutput, calls=%fused_computation.6 | convolution fusion | flops 268566528 | bytes 8716288 | tf_op jit(solution)/shard_map/dot_general | solution.py:128
  123.6 4.0 %all-to-all-start = ((bf16[4,32,1024]{2,1,0:T(8,128)(2,1)}), bf16[4,32,1024]{2,1,0:T(8,128)(2,1)S(1)}, u32[]{:S(2)}, u32[]{:S(2)}) async-start(bf16[4,32,1024]{2,1,0:T(8,128)(2,1)} %bitcast.198), calls=%async_computation | async-start | bytes 524288 | tf_op jit(solution)/shard_map/all_to_all | solution.py:19
  128.6 5.0 %all-to-all-done = bf16[4,32,1024]{2,1,0:T(8,128)(2,1)S(1)} async-done(((bf16[4,32,1024]{2,1,0:T(8,128)(2,1)}), bf16[4,32,1024]{2,1,0:T(8,128)(2,1)S(1)}, u32[]{:S(2)}, u32[]{:S(2)}) %all-to-all-start) | async-done | bytes 262176 | tf_op jit(solution)/shard_map/all_to_all | solution.py:19
  134.6 7.1 %psum.7 = f32[32]{0:T(128)S(1)} all-reduce(f32[32]{0:T(128)S(1)} %reduce_sum.96), channel_id=1, replica_groups=mesh['groups'=2,'dp'=32,'expert'=4] {'expert'}, use_global_device_ids=true, to_apply=%region_14.15 | all-reduce | flops 32 | bytes 256 | tf_op jit(solution)/shard_map/psum | solution.py:136
  142.6 2.3 convolution_convert_fusion.3
  145.0 3.6 reshape.165
  148.6 3.1 copy.146
  151.7 78.1 %all_to_all.20 = bf16[2,32,10,1024]{3,0,2,1:T(2,128)(2,1)S(1)} all-to-all(bf16[2,32,10,1024]{3,0,2,1:T(2,128)(2,1)S(1)} %copy.146), channel_id=1, replica_groups=mesh['groups'=2,'dp'=32,'expert'=4] {'dp'}, dimensions={1} | all-to-all | bytes 2621440 | tf_op jit(solution)/shard_map/all_to_all | solution.py:154
  229.8 3.2 fusion.13
  234.2 1.4 pad_maximum_fusion
  235.7 4.1 %copy.151 = bf16[4,320,768]{1,2,0:T(8,128)(2,1)} copy(bf16[4,320,768]{2,1,0:T(8,128)(2,1)} %pad_maximum_fusion) | data formatting | bytes 3932160 | tf_op jit(solution)/shard_map/concatenate | solution.py:24
  239.8 1.9 copy.152
  241.7 31.3 %all_to_all.21 = bf16[4,4,320,192]{2,3,1,0:T(8,128)(2,1)S(1)} all-to-all(bf16[4,4,320,192]{2,3,1,0:T(8,128)(2,1)S(1)} %copy.152), channel_id=1, replica_groups=mesh['groups'=2,'dp'=32,'expert'=4] {'expert'}, dimensions={0} | all-to-all | bytes 3932160 | tf_op jit(solution)/shard_map/all_to_all | solution.py:19
  273.6 12.4 %all_gather.7 = bf16[2,320,768]{1,2,0:T(8,128)(2,1)S(1)} all-gather(bf16[2,320,192]{1,2,0:T(8,128)(2,1)S(1)} %fusion.51), channel_id=1, replica_groups=mesh['groups'=2,'dp'=32,'expert'=4] {'expert'}, dimensions={2}, use_global_device_ids=true | all-gather | bytes 1228800 | tf_op jit(solution)/shard_map/all_gather | solution.py:166
  286.0 1.2 convolution_convert_fusion.2
  287.3 2.4 copy.153
  289.7 9.1 %all-to-all-start.3 = ((bf16[2,32,10,1024]{3,0,2,1:T(2,128)(2,1)}), bf16[2,32,10,1024]{3,0,2,1:T(2,128)(2,1)}, u32[]{:S(2)}, u32[]{:S(2)}) async-start(bf16[2,32,10,1024]{3,0,2,1:T(2,128)(2,1)} %bitcast.193), calls=%async_computation.3 | async-start | bytes 2621440 | tf_op jit(solution)/shard_map/all_to_all | solution.py:171
  299.0 66.6 %all-to-all-done.3 = bf16[2,32,10,1024]{3,0,2,1:T(2,128)(2,1)} async-done(((bf16[2,32,10,1024]{3,0,2,1:T(2,128)(2,1)}), bf16[2,32,10,1024]{3,0,2,1:T(2,128)(2,1)}, u32[]{:S(2)}, u32[]{:S(2)}) %all-to-all-start.3) | async-done | bytes 1310752 | tf_op jit(solution)/shard_map/all_to_all | solution.py:171
  365.6 3.2 copy.154
  368.8 3.6 reshape.169
  372.4 3.9 %gather_fusion = bf16[256,1024]{1,0:T(8,128)(2,1)} fusion(bf16[640,1024]{1,0:T(8,128)(2,1)} %reshape.169, s32[1024]{0:T(1024)S(1)} %pad_clamp_fusion), kind=kCustom, calls=%fused_computation | custom fusion | bytes 1049600 | tf_op jit(solution)/shard_map/gather | solution.py:173
  376.3 1.4 fusion.49
  (63 shorter events, 19.2 us)
Async XLA Ops:
  6.5 279.4 %copy-start = (bf16[2,768,1024]{2,1,0:T(8,128)(2,1)S(1)}, bf16[2,768,1024]{2,1,0:T(8,128)(2,1)}, u32[]{:S(2)}) copy-start(bf16[2,768,1024]{2,1,0:T(8,128)(2,1)} %param.23) | copy-start | bytes 9437188
  6.6 111.4 %all-gather.2.cloned.1.call-start = ((), (), s32[]{:S(2)}) async-start(), calls=%async_computation.4 | async-start | bytes 8650752 | tf_op jit(solution)/shard_map/all_gather | solution.py:130
  13.3 6.1 %copy-start.4 = (bf16[2,16,1,256]{3,1,2,0:T(8,128)(2,1)S(1)}, bf16[2,16,1,256]{3,1,2,0:T(8,128)(2,1)}, u32[]{:S(2)}) copy-start(bf16[2,16,1,256]{3,1,2,0:T(8,128)(2,1)} %param.13) | copy-start | bytes 49156
  21.9 0.6 copy-start.2
  37.0 1.7 copy-start.5
  123.6 9.9 %all-to-all-start = ((bf16[4,32,1024]{2,1,0:T(8,128)(2,1)}), bf16[4,32,1024]{2,1,0:T(8,128)(2,1)S(1)}, u32[]{:S(2)}, u32[]{:S(2)}) async-start(bf16[4,32,1024]{2,1,0:T(8,128)(2,1)} %bitcast.198), calls=%async_computation | async-start | bytes 524288 | tf_op jit(solution)/shard_map/all_to_all | solution.py:19
  148.6 84.4 %slice-start = ((s8[6291456]{0:T(1024)(128)(4,1)}), s8[2097152]{0:T(1024)(128)(4,1)S(1)}, s32[]{:S(2)}) async-start(s8[6291456]{0:T(1024)(128)(4,1)} %bitcast.203), calls=%async_computation.5 | async-start | bytes 4194304
  229.8 3.2 slice-start.1
  287.2 11.6 %copy-start.3 = (f32[2,16,8]{1,2,0:T(8,128)S(1)}, f32[2,16,8]{1,2,0:T(8,128)}, u32[]{:S(2)}) copy-start(f32[2,16,8]{1,2,0:T(8,128)} %param.21) | copy-start | bytes 3076
  289.7 75.9 %all-to-all-start.3 = ((bf16[2,32,10,1024]{3,0,2,1:T(2,128)(2,1)}), bf16[2,32,10,1024]{3,0,2,1:T(2,128)(2,1)}, u32[]{:S(2)}, u32[]{:S(2)}) async-start(bf16[2,32,10,1024]{3,0,2,1:T(2,128)(2,1)} %bitcast.193), calls=%async_computation.3 | async-start | bytes 2621440 | tf_op jit(solution)/shard_map/all_to_all | solution.py:171
  372.4 5.3 %copy-start.1 = (bf16[2,16,1024]{2,1,0:T(8,128)(2,1)S(1)}, bf16[2,16,1024]{2,1,0:T(8,128)(2,1)}, u32[]{:S(2)}) copy-start(bf16[2,16,1024]{2,1,0:T(8,128)(2,1)} %param.17) | copy-start | bytes 196612
Sparse Core Ops, SparseCore 0:
  9.1 108.8 all-gather.1
where the time goes:
time: 387 us; the launch traced here: 385 us
  waiting for transfers between devices  149 us (39%)
  blocking collectives  129 us (33%)
  local copies, waits for them, and re-layouts  35.8 us (9%)
  matrix products  27.9 us (7%)
  other arithmetic  17 us (4%)
  between operations  13.7 us (4%)
  starting transfers between devices  13.1 us (3%)
    all_to_all x1, blocking collectives, body(): lax.all_to_all(outgoing, 'dp', split_axis=1, concat_axis=1, tiled=True)  78.1 us
    all_gather x1, waiting for transfers between devices, body(): lax.all_gather(out_weight, 'dp', axis=1, tiled=True)  76.4 us
    all_to_all x1, waiting for transfers between devices, body(): lax.all_to_all(expert_out, 'dp', split_axis=1, concat_axis=1, tiled=True)  66.6 us
    all_to_all x1, blocking collectives, summed_on_arrival(): lax.all_to_all(in_blocks(array, dim, length), axis, 0, 0, tiled=True)  31.3 us
    all_gather x1, blocking collectives, body(): activated = lax.all_gather(active_share, 'expert', axis=2, tiled=True)  12.4 us
    all_to_all x1, starting transfers between devices, body(): lax.all_to_all(expert_out, 'dp', split_axis=1, concat_axis=1, tiled=True)  9.08 us
  transfers between devices with their start and end apart: 3, of which 3 were waited for; matrix products, arithmetic and copies ran while one was open for 9% of the time, Pallas kernels for 0%

commit v1 on v0

--- a/solution.py
+++ b/solution.py
@@ -7,6 +7,13 @@
 NEG = -1e30
 EPS = 1e-06
 EXACT = lax.Precision.HIGHEST
+
+
+def gather_over(array, axis, d):
+    size = lax.axis_size(axis)
+    parts = jnp.stack([array for _ in range(size)])
+    parts = lax.all_to_all(parts, axis, split_axis=0, concat_axis=0)
+    return jnp.concatenate(parts, axis=d)
 
 
 def in_blocks(array, dim, length):
@@ -126,9 +133,7 @@
     step_count, req_count, head_cols = attended.shape
     flat_attended = attended.reshape(step_count * req_count, head_cols)
     partial_out = jnp.dot(
-        flat_attended,
-        lax.all_gather(out_weight, "dp", axis=1, tiled=True),
-        preferred_element_type=jnp.float32,
+        flat_attended, gather_over(out_weight, "dp", 1), preferred_element_type=jnp.float32
     )
     projected = summed_on_arrival(partial_out.astype(jnp.bfloat16), "expert", 1)
     quarter = projected.shape[1]

time: 387 us -> 660 us (1.71)
  waiting for transfers between devices: 149 us -> 397 us
  starting transfers between devices: 13.1 us -> 39.2 us
  between operations: 13.7 us -> 0.35 us
  local copies, waits for them, and re-layouts: 35.8 us -> 42.4 us
    all_to_all x0 -> x1, waiting for transfers between devices: none -> 327 us  [gather_over(): parts = lax.all_to_all(parts, axis, split_axis=0, concat_axis=0)]
    all_gather x1 -> x0, waiting for transfers between devices: 76.4 us -> none  [body(): lax.all_gather(out_weight, 'dp', axis=1, tiled=True)]
    all_to_all x0 -> x1, starting transfers between devices: none -> 25.6 us  [gather_over(): parts = lax.all_to_all(parts, axis, split_axis=0, concat_axis=0)]
  transfers between devices with their start and end apart: 3 -> 3, of which waited for: 3 -> 3; matrix products, arithmetic and copies ran while one was open for 9% -> 5% of each run, Pallas kernels for 0% -> 0%
where the time goes in v1:
time: 660 us; the launch traced here: 658 us
  waiting for transfers between devices  397 us (60%)
  blocking collectives  134 us (20%)
  local copies, waits for them, and re-layouts  42.4 us (6%)
  starting transfers between devices  39.2 us (6%)
  matrix products  28.1 us (4%)
  other arithmetic  16.9 us (3%)
    all_to_all x1, waiting for transfers between devices, gather_over(): parts = lax.all_to_all(parts, axis, split_axis=0, concat_axis=0)  327 us
    all_to_all x1, blocking collectives, body(): lax.all_to_all(outgoing, 'dp', split_axis=1, concat_axis=1, tiled=True)  83.5 us
    all_to_all x1, waiting for transfers between devices, body(): lax.all_to_all(expert_out, 'dp', split_axis=1, concat_axis=1, tiled=True)  66.6 us
    all_to_all x1, blocking collectives, summed_on_arrival(): lax.all_to_all(in_blocks(array, dim, length), axis, 0, 0, tiled=True)  31.3 us
    all_to_all x1, starting transfers between devices, gather_over(): parts = lax.all_to_all(parts, axis, split_axis=0, concat_axis=0)  25.6 us
  transfers between devices with their start and end apart: 3, of which 3 were waited for; matrix products, arithmetic and copies ran while one was open for 5% of the time, Pallas kernels for 0%

profile of v1, /device:TPU:33, one launch (start us, length us, event | category | flops | bytes accessed | tf_op | source)
XLA Modules:
  0.0 658.3 jit_solution(16739225165646645850)
XLA Ops:
  1.2 4.3 stack.2
  5.5 25.6 %all-to-all-start = ((bf16[32,1024,128]{1,2,0:T(8,128)(2,1)}), bf16[32,1024,128]{1,2,0:T(8,128)(2,1)}, u32[]{:S(2)}, u32[]{:S(2)}) async-start(bf16[32,1024,128]{1,2,0:T(8,128)(2,1)} %stack.2), calls=%async_computation | async-start | bytes 16777216 | tf_op jit(solution)/shard_map/all_to_all | solution.py:15
  31.6 2.4 gather_fusion.1
  36.1 1.5 select_reduce_fusion
  38.3 4.4 fusion.12
  45.6 1.9 fusion.86
  49.8 3.9 fusion.10
  53.7 1.7 copy.135
  60.1 3.0 fusion.20
  63.2 1.7 fusion.42
  64.9 326.6 %all-to-all-done = bf16[32,1024,128]{1,2,0:T(8,128)(2,1)} async-done(((bf16[32,1024,128]{1,2,0:T(8,128)(2,1)}), bf16[32,1024,128]{1,2,0:T(8,128)(2,1)}, u32[]{:S(2)}, u32[]{:S(2)}) %all-to-all-start) | async-done | bytes 8388640 | tf_op jit(solution)/shard_map/all_to_all | solution.py:15
  391.4 5.9 convolution_convert_fusion
  398.1 4.5 all-to-all-start.1
  404.1 4.2 all-to-all-done.1
  409.4 6.9 %psum.7 = f32[32]{0:T(128)S(1)} all-reduce(f32[32]{0:T(128)S(1)} %reduce_sum.96), channel_id=1, replica_groups=mesh['groups'=2,'dp'=32,'expert'=4] {'expert'}, use_global_device_ids=true, to_apply=%region_14.15 | all-reduce | flops 32 | bytes 256 | tf_op jit(solution)/shard_map/psum | solution.py:141
  417.2 2.3 convolution_convert_fusion.3
  419.5 3.6 reshape.175
  423.1 3.1 copy.150
  426.2 83.5 %all_to_all.25 = bf16[2,32,10,1024]{3,0,2,1:T(2,128)(2,1)S(1)} all-to-all(bf16[2,32,10,1024]{3,0,2,1:T(2,128)(2,1)S(1)} %copy.150), channel_id=1, replica_groups=mesh['groups'=2,'dp'=32,'expert'=4] {'dp'}, dimensions={1} | all-to-all | bytes 2621440 | tf_op jit(solution)/shard_map/all_to_all | solution.py:159
  509.7 3.2 fusion.16
  514.1 1.4 pad_maximum_fusion
  515.6 4.1 copy.155
  519.7 1.9 copy.156
  521.6 31.3 %all_to_all.26 = bf16[4,4,320,192]{2,3,1,0:T(8,128)(2,1)S(1)} all-to-all(bf16[4,4,320,192]{2,3,1,0:T(8,128)(2,1)S(1)} %copy.156), channel_id=1, replica_groups=mesh['groups'=2,'dp'=32,'expert'=4] {'expert'}, dimensions={0} | all-to-all | bytes 3932160 | tf_op jit(solution)/shard_map/all_to_all | solution.py:26
  553.5 12.4 %all_gather.3 = bf16[2,320,768]{1,2,0:T(8,128)(2,1)S(1)} all-gather(bf16[2,320,192]{1,2,0:T(8,128)(2,1)S(1)} %fusion.51), channel_id=1, replica_groups=mesh['groups'=2,'dp'=32,'expert'=4] {'expert'}, dimensions={2}, use_global_device_ids=true | all-gather | bytes 1228800 | tf_op jit(solution)/shard_map/all_gather | solution.py:171
  567.2 2.4 copy.157
  569.6 9.1 %all-to-all-start.4 = ((bf16[2,32,10,1024]{3,0,2,1:T(2,128)(2,1)}), bf16[2,32,10,1024]{3,0,2,1:T(2,128)(2,1)}, u32[]{:S(2)}, u32[]{:S(2)}) async-start(bf16[2,32,10,1024]{3,0,2,1:T(2,128)(2,1)} %bitcast.196), calls=%async_computation.4 | async-start | bytes 2621440 | tf_op jit(solution)/shard_map/all_to_all | solution.py:176
  578.9 66.6 %all-to-all-done.4 = bf16[2,32,10,1024]{3,0,2,1:T(2,128)(2,1)} async-done(((bf16[2,32,10,1024]{3,0,2,1:T(2,128)(2,1)}), bf16[2,32,10,1024]{3,0,2,1:T(2,128)(2,1)}, u32[]{:S(2)}, u32[]{:S(2)}) %all-to-all-start.4) | async-done | bytes 1310752 | tf_op jit(solution)/shard_map/all_to_all | solution.py:176
  645.5 3.2 copy.158
  648.7 3.6 reshape.179
  652.3 3.9 gather_fusion
  656.2 1.4 fusion.49
  (74 shorter events, 22.4 us)
Async XLA Ops:
  0.0 565.9 %copy-start = (bf16[2,768,1024]{2,1,0:T(8,128)(2,1)S(1)}, bf16[2,768,1024]{2,1,0:T(8,128)(2,1)}, u32[]{:S(2)}) copy-start(bf16[2,768,1024]{2,1,0:T(8,128)(2,1)} %param.23) | copy-start | bytes 9437188
  5.5 25.6 %copy-start.9 = (s32[2,16,8]{1,2,0:T(8,128)S(1)}, s32[2,16,8]{1,2,0:T(8,128)}, u32[]{:S(2)}) copy-start(s32[2,16,8]{1,2,0:T(8,128)} %param.20) | copy-start | bytes 3076
  5.5 385.9 %all-to-all-start = ((bf16[32,1024,128]{1,2,0:T(8,128)(2,1)}), bf16[32,1024,128]{1,2,0:T(8,128)(2,1)}, u32[]{:S(2)}, u32[]{:S(2)}) async-start(bf16[32,1024,128]{1,2,0:T(8,128)(2,1)} %stack.2), calls=%async_computation | async-start | bytes 16777216 | tf_op jit(solution)/shard_map/all_to_all | solution.py:15
  31.5 3.2 copy-start.8
  31.5 4.5 copy-start.10
  31.5 6.2 copy-start.6
  47.5 0.6 copy-start.3
  56.2 0.6 copy-start.2
  391.4 11.2 %copy-start.4 = (s32[2,16,8]{2,1,0:T(8,128)S(1)}, s32[2,16,8]{2,1,0:T(8,128)}, u32[]{:S(2)}) copy-start(s32[2,16,8]{2,1,0:T(8,128)} %reshape.191) | copy-start | bytes 3076
  398.1 10.2 %all-to-all-start.1 = ((bf16[4,32,1024]{2,1,0:T(8,128)(2,1)}), bf16[4,32,1024]{2,1,0:T(8,128)(2,1)S(1)}, u32[]{:S(2)}, u32[]{:S(2)}) async-start(bf16[4,32,1024]{2,1,0:T(8,128)(2,1)} %bitcast.201), calls=%async_computation.1 | async-start | bytes 524288 | tf_op jit(solution)/shard_map/all_to_all | solution.py:26
  423.1 89.8 %slice-start = ((s8[6291456]{0:T(1024)(128)(4,1)}), s8[2097152]{0:T(1024)(128)(4,1)S(1)}, s32[]{:S(2)}) async-start(s8[6291456]{0:T(1024)(128)(4,1)} %bitcast.206), calls=%async_computation.5 | async-start | bytes 4194304
  509.7 3.2 slice-start.1
  567.2 11.5 %copy-start.7 = (f32[2,16,8]{1,2,0:T(8,128)S(1)}, f32[2,16,8]{1,2,0:T(8,128)}, u32[]{:S(2)}) copy-start(f32[2,16,8]{1,2,0:T(8,128)} %param.21) | copy-start | bytes 3076
  567.2 11.6 %copy-start.5 = (s32[2,16,8]{2,1,0:T(8,128)S(1)}, s32[2,16,8]{2,1,0:T(8,128)}, u32[]{:S(2)}) copy-start(s32[2,16,8]{2,1,0:T(8,128)} %get-tuple-element.5) | copy-start | bytes 3076
  569.6 75.9 %all-to-all-start.4 = ((bf16[2,32,10,1024]{3,0,2,1:T(2,128)(2,1)}), bf16[2,32,10,1024]{3,0,2,1:T(2,128)(2,1)}, u32[]{:S(2)}, u32[]{:S(2)}) async-start(bf16[2,32,10,1024]{3,0,2,1:T(2,128)(2,1)} %bitcast.196), calls=%async_computation.4 | async-start | bytes 2621440 | tf_op jit(solution)/shard_map/all_to_all | solution.py:176
  652.3 5.3 copy-start.1
